TPU v7x, 128 devices: a whole 4x4x4 slice. The times are simulated.
128 devices in a mesh: dp: 8 (over x, core), mp: 16 (over y, z).
Axes of the slice: x: 4, y: 4, z: 4, core: 2. Of those that a mesh axis runs over, the one named last changes fastest.
Arguments:
- tokens: bfloat16 [256, 8192], P('dp', 'mp'), may hold values from -6 to 6
- gate_up_weight: bfloat16 [2, 8192, 15360], P(None, 'mp', 'dp'), may hold values from -0.0625 to 0.0625
- down_weight: bfloat16 [15360, 8192], P('dp', 'mp'), may hold values from -0.046875 to 0.046875
- gate_up_input_factor: bfloat16 [2, 8192, 64], P(None, 'mp'), may hold values from -0.0625 to 0.0625
- gate_up_output_factor: bfloat16 [2, 64, 15360], P(None, None, 'dp'), may hold values from -0.046875 to 0.046875
- down_input_factor: bfloat16 [15360, 64], P('dp'), may hold values from -0.046875 to 0.046875
- down_output_factor: bfloat16 [64, 8192], P(None, 'mp'), may hold values from -0.0625 to 0.0625
- cotangent: bfloat16 [256, 8192], P('dp', 'mp'), may hold values from -6 to 6
Outputs:
- output: bfloat16 [256, 8192], P('dp', 'mp')
- input_grad: bfloat16 [256, 8192], P('dp', 'mp')
- grad_gate_up_lower: float32 [2, 8192, 64], P(None, 'mp')
- gate_up_output_factor_gradient: float32 [2, 64, 15360], P(None, None, 'dp')
- down_input_factor_gradient: float32 [15360, 64], P('dp')
- down_output_factor_gradient: float32 [64, 8192], P(None, 'mp')
All inputs are finite; a program needn't handle non-finite values.
Results may differ from a plain program's by a relative error of at most 0.0065.
Values may be sent and summed in bfloat16 or wider, within the bound.
A program may use at most 64 MiB of HBM per device.

v0:
```python
import jax
import jax.numpy as jnp
from jax import lax
from jax.sharding import Mesh
from jax.sharding import PartitionSpec as P

MP = ("mp_0", "mp_1")
adapter_scale = 2.0


def sent_to_all(array, axis):
    length = lax.axis_size(axis)
    return lax.all_to_all(
        jnp.broadcast_to(array[None], (length, *array.shape)), axis, 0, 0, tiled=True
    )


def joined_along(parts, dim):
    shape = list(parts.shape[1:])
    shape[dim] *= parts.shape[0]
    return jnp.moveaxis(parts, 0, dim).reshape(shape)


def gathered_copies(array, axis, dim):
    parts = sent_to_all(array, axis)
    return joined_along(parts, dim)


def cut_along(array, dim, length):
    shape = array.shape
    parts = array.reshape(*shape[:dim], length, shape[dim] // length, *shape[dim + 1 :])
    return jnp.moveaxis(parts, dim, 0)


def piece_ends(length, count):
    hop = length // count
    if hop >= 8:
        hop -= hop % 8
    return [hop * k for k in range(1, count)]


def sum_in_order(parts, axes, turns):
    shape = [lax.axis_size(a) for a in axes]
    parts = parts.reshape(*shape, *parts.shape[1:])
    parts = parts.transpose(*turns, *range(len(axes), parts.ndim))
    parts = parts.reshape(-1, *parts.shape[len(axes) :])
    for k in turns:
        parts = lax.psum_scatter(parts, axes[k], scatter_dimension=0, tiled=True)
    return parts[0]


def sum_at_once(array, axes, dim):
    parts = cut_along(array, dim, lax.axis_size(axes))
    widest = max(range(1, max(2, parts.ndim - 1)), key=lambda d: parts.shape[d])
    count, finished = (len(axes), [])
    for first, section in enumerate(
        jnp.split(parts, piece_ends(parts.shape[widest], count), axis=widest)
    ):
        if section.size:
            turns = [(first + k) % count for k in range(count)]
            finished.append(sum_in_order(section, axes, turns))
    return jnp.concatenate(finished, axis=widest - 1)


def sum_at_owner(array, axis, dim):
    parts = cut_along(array, dim, lax.axis_size(axis))
    arrived = lax.all_to_all(parts, axis, split_axis=0, concat_axis=0, tiled=True)
    return arrived.sum(axis=0)


def over_copies(array, axis):
    return sent_to_all(array, axis).sum(axis=0)


def in_one(arrays, axis):
    ravelled, at, finished = (jnp.concatenate([a.reshape(-1) for a in arrays]), 0, [])
    so_far = over_copies(ravelled, axis)
    for a in arrays:
        finished.append(so_far[at : at + a.size].reshape(a.shape))
        at += a.size
    return tuple(finished)


def contract_trailing(left, right, matmul_precision=None):
    return lax.dot_general(
        left,
        right,
        (((1,), (1,)), ((), ())),
        preferred_element_type=jnp.float32,
        precision=matmul_precision,
    )


def contract_leading(left, right, matmul_precision=None):
    return lax.dot_general(
        left,
        right,
        (((0,), (0,)), ((), ())),
        preferred_element_type=jnp.float32,
        precision=matmul_precision,
    )


def per_device(
    tokens,
    gate_up_weight,
    down_weight,
    gate_up_input_factor,
    gate_up_output_factor,
    down_input_factor,
    down_output_factor,
    cotangent,
):
    single_float = jnp.float32
    product_precision = lax.Precision.DEFAULT
    tok_rows = tokens.shape[0]
    input_rows_full = gathered_copies(tokens, "dp", 0)
    total = input_rows_full.shape[0]
    mp_rows = total // lax.axis_size(MP)
    scale_factor = total ** (-0.5)
    mp_start = lax.axis_index(MP) * mp_rows
    dp_start = lax.axis_index("dp") * tok_rows
    low_part = jnp.einsum(
        "td,kdr->tkr", input_rows_full, gate_up_input_factor, preferred_element_type=single_float
    )
    upper_widened = gate_up_output_factor.astype(single_float)
    term = jnp.einsum(
        "td,kdf->tkf", input_rows_full, gate_up_weight, preferred_element_type=single_float
    )
    low_slab = low_part
    term = term + adapter_scale * jnp.einsum("ubw,bwa->uba", low_slab, upper_widened)
    preactivation = sum_at_once(term, MP, 0)
    gate = preactivation[:, 0]
    upper = preactivation[:, 1]
    hidden_state = (jax.nn.silu(gate) * upper).astype(jnp.bfloat16)
    hidden_state_full = gathered_copies(hidden_state, MP, 0)
    low_down_part = jnp.dot(
        hidden_state_full, down_input_factor, preferred_element_type=single_float
    )
    down_widened_rows = down_output_factor.astype(single_float)
    term = jnp.dot(hidden_state_full, down_weight, preferred_element_type=single_float)
    low_slab = low_down_part
    term = term + adapter_scale * jnp.dot(low_slab, down_widened_rows)
    output = sum_at_owner(term, "dp", 0)
    output = output.astype(jnp.bfloat16)
    cot_all = gathered_copies(cotangent, "dp", 0)
    coeff_part = contract_leading(
        low_down_part, cot_all.astype(single_float), matmul_precision=product_precision
    )
    backward_down_rows = over_copies(contract_trailing(cot_all, down_output_factor), MP).astype(
        jnp.bfloat16
    )
    hidden_state_gradient = lax.psum_scatter(
        contract_trailing(cot_all, down_weight), MP, scatter_dimension=0, tiled=True
    )
    backward_row_block = lax.dynamic_slice_in_dim(backward_down_rows, mp_start, mp_rows, 0)
    hidden_state_gradient = hidden_state_gradient + adapter_scale * contract_trailing(
        backward_row_block, down_input_factor
    )
    down_input_factor_gradient = (
        adapter_scale * scale_factor * contract_leading(hidden_state_full, backward_down_rows)
    )
    sigma = jax.nn.sigmoid(gate)
    gate_back = hidden_state_gradient * upper * sigma * (1.0 + gate * (1.0 - sigma))
    up_back = hidden_state_gradient * gate * sigma
    pre_back = jnp.stack([gate_back, up_back], axis=1).astype(jnp.bfloat16)
    back_all = gathered_copies(pre_back, MP, 0)
    upper_partial = jnp.einsum("tkr,tkf->krf", low_part, back_all.astype(single_float))
    gate_up_output_factor_gradient = adapter_scale * scale_factor * lax.psum(upper_partial, MP)
    back_low_part = jnp.einsum(
        "tkf,krf->tkr", back_all, gate_up_output_factor, preferred_element_type=single_float
    )
    back_low_sum, down_coefficient = in_one((back_low_part, coeff_part), "dp")
    down_output_factor_gradient = adapter_scale * scale_factor * down_coefficient
    backward_lower_rows = back_low_sum.astype(jnp.bfloat16)
    grad_gate_up_lower = (
        adapter_scale
        * scale_factor
        * jnp.einsum(
            "qi,qps->pis", input_rows_full, backward_lower_rows, preferred_element_type=single_float
        )
    )
    input_total_sum = sum_at_owner(
        jnp.einsum("tkf,kdf->td", back_all, gate_up_weight, preferred_element_type=single_float),
        "dp",
        0,
    )
    low_rows_back = lax.dynamic_slice_in_dim(backward_lower_rows, dp_start, tok_rows, 0)
    input_total_sum = input_total_sum + adapter_scale * jnp.einsum(
        "tkr,kdr->td", low_rows_back, gate_up_input_factor, preferred_element_type=single_float
    )
    input_grad = input_total_sum.astype(jnp.bfloat16)
    return (
        output,
        input_grad,
        grad_gate_up_lower,
        gate_up_output_factor_gradient,
        down_input_factor_gradient,
        down_output_factor_gradient,
    )


def solution(mesh):
    torus = Mesh(mesh.devices.reshape(mesh.shape["dp"], 4, 4), ("dp", "mp_0", "mp_1"))
    in_specs = (
        P("dp", MP),
        P(None, MP, "dp"),
        P("dp", MP),
        P(None, MP, None),
        P(None, None, "dp"),
        P("dp", None),
        P(None, MP),
        P("dp", MP),
    )
    out_specs = (
        P("dp", MP),
        P("dp", MP),
        P(None, MP, None),
        P(None, None, "dp"),
        P("dp", None),
        P(None, MP),
    )
    return jax.shard_map(
        per_device, mesh=torus, in_specs=in_specs, out_specs=out_specs, check_vma=False
    )
```

profile of v0, /device:TPU:0, one launch (start us, length us, event | category | flops | bytes accessed | tf_op | source)
XLA Modules:
  0.0 345.4 jit_solution(7605972328173418897)
XLA Ops:
  9.0 11.7 %all_to_all.41 = bf16[8,32,512]{2,1,0:T(8,128)(2,1)S(1)} all-to-all(bf16[8,32,512]{2,1,0:T(8,128)(2,1)S(1)} %broadcast_in_dim.12), channel_id=1, replica_groups=mesh['dp'=8,'mp_0'=4,'mp_1'=4] {'dp'}, dimensions={0} | all-to-all | bytes 524288 | tf_op jit(solution)/shard_map/all_to_all | solution.py:13
  20.7 3.4 fusion.22
  28.1 3.0 copy.52
  31.8 9.9 %all_to_all.42 = bf16[8,32,512]{2,1,0:T(8,128)(2,1)S(1)} all-to-all(bf16[8,32,512]{2,1,0:T(8,128)(2,1)S(1)} %broadcast_in_dim.14), channel_id=1, replica_groups=mesh['dp'=8,'mp_0'=4,'mp_1'=4] {'dp'}, dimensions={0} | all-to-all | bytes 524288 | tf_op jit(solution)/shard_map/all_to_all | solution.py:13
  43.8 14.1 %reduce-scatter.9.cloned.1.call-done = f32[4,8,2,1920]{3,1,2,0:T(8,128)} async-done(((f32[16,8,2,1920]{3,1,2,0:T(8,128)}), f32[4,8,2,1920]{3,1,2,0:T(8,128)}) %reduce-scatter.9.cloned.1.call-update) | async-done | bytes 491536 | tf_op jit(solution)/shard_map/reduce_scatter | solution.py:48
  59.3 5.5 %all-to-all-start.4 = ((f32[16,256,64]{1,2,0:T(8,128)}), f32[16,256,64]{1,2,0:T(8,128)}, u32[]{:S(2)}, u32[]{:S(2)}) async-start(f32[16,256,64]{1,2,0:T(8,128)} %broadcast_in_dim.15), calls=%async_computation.8 | async-start | bytes 2097152 | tf_op jit(solution)/shard_map/all_to_all | solution.py:13
  64.8 32.6 %reduce-scatter.5.cloned.1.call-done = f32[4,8,2,1920]{3,1,2,0:T(8,128)} async-done(((f32[16,8,2,1920]{3,1,2,0:T(8,128)}), f32[4,8,2,1920]{3,1,2,0:T(8,128)}) %reduce-scatter.5.cloned.1.call-update) | async-done | bytes 491536 | tf_op jit(solution)/shard_map/reduce_scatter | solution.py:48
  99.9 46.6 %all-reduce.6.cloned.1.call-done = f32[256,1920]{1,0:T(8,128)} async-done(((f32[256,1920]{1,0:T(8,128)}), f32[256,1920]{1,0:T(8,128)}) %all-reduce.6.cloned.1.call-update) | async-done | bytes 1966096
  146.5 2.1 fusion.15
  149.6 4.9 %all-to-all-start.1 = ((bf16[16,16,1920]{2,1,0:T(8,128)(2,1)}), bf16[16,16,1920]{2,1,0:T(8,128)(2,1)S(1)}, u32[]{:S(2)}, u32[]{:S(2)}) async-start(bf16[16,16,1920]{2,1,0:T(8,128)(2,1)} %broadcast_in_dim.13), calls=%async_computation.5 | async-start | bytes 1966080 | tf_op jit(solution)/shard_map/all_to_all | solution.py:13
  156.1 14.7 %all-to-all-done.1 = bf16[16,16,1920]{2,1,0:T(8,128)(2,1)S(1)} async-done(((bf16[16,16,1920]{2,1,0:T(8,128)(2,1)}), bf16[16,16,1920]{2,1,0:T(8,128)(2,1)S(1)}, u32[]{:S(2)}, u32[]{:S(2)}) %all-to-all-start.1) | async-done | bytes 983072 | tf_op jit(solution)/shard_map/all_to_all | solution.py:13
  170.8 2.3 broadcast_in_dim.16
  173.1 4.4 %all-to-all-start.5 = ((bf16[16,16,2,1920]{3,1,2,0:T(8,128)(2,1)}), bf16[16,16,2,1920]{3,1,2,0:T(8,128)(2,1)}, u32[]{:S(2)}, u32[]{:S(2)}) async-start(bf16[16,16,2,1920]{3,1,2,0:T(8,128)(2,1)} %broadcast_in_dim.16), calls=%async_computation.9 | async-start | bytes 3932160 | tf_op jit(solution)/shard_map/all_to_all | solution.py:13
  181.5 22.5 %all-to-all-done.5 = bf16[16,16,2,1920]{3,1,2,0:T(8,128)(2,1)} async-done(((bf16[16,16,2,1920]{3,1,2,0:T(8,128)(2,1)}), bf16[16,16,2,1920]{3,1,2,0:T(8,128)(2,1)}, u32[]{:S(2)}, u32[]{:S(2)}) %all-to-all-start.5) | async-done | bytes 1966112 | tf_op jit(solution)/shard_map/all_to_all | solution.py:13
  204.0 4.3 %all-to-all-start.2 = ((f32[8,32,512]{2,1,0:T(8,128)}), f32[8,32,512]{2,1,0:T(8,128)}, u32[]{:S(2)}, u32[]{:S(2)}) async-start(f32[8,32,512]{2,1,0:T(8,128)} %bitcast.110), calls=%async_computation.6 | async-start | bytes 1048576 | tf_op jit(solution)/shard_map/all_to_all | solution.py:67
  214.5 4.7 %fusion.3 = f32[8,32,512]{2,1,0:T(8,128)} fusion(bf16[8,32,1920,2]{2,1,0,3:T(8,128)(2,1)} %bitcast.96, bf16[2,512,1920]{2,1,0:T(8,128)(2,1)} %param.9), kind=kOutput, calls=%fused_computation.6 | convolution fusion | flops 1006632960 | bytes 6422528 | tf_op jit(solution)/shard_map/tkf,kdf->td/dot_general | solution.py:184
  219.3 4.8 %all-to-all-start.6 = ((f32[8,32,512]{2,1,0:T(8,128)}), f32[8,32,512]{2,1,0:T(8,128)}, u32[]{:S(2)}, u32[]{:S(2)}) async-start(f32[8,32,512]{2,1,0:T(8,128)} %fusion.3), calls=%async_computation.10 | async-start | bytes 1048576 | tf_op jit(solution)/shard_map/all_to_all | solution.py:67
  225.0 9.4 %all-to-all-done.6 = f32[8,32,512]{2,1,0:T(8,128)} async-done(((f32[8,32,512]{2,1,0:T(8,128)}), f32[8,32,512]{2,1,0:T(8,128)}, u32[]{:S(2)}, u32[]{:S(2)}) %all-to-all-start.6) | async-done | bytes 524320 | tf_op jit(solution)/shard_map/all_to_all | solution.py:67
  234.5 2.4 broadcast_in_dim.17
  236.9 4.5 %all-to-all-start.7 = ((f32[8,1,65536]{2,1,0:T(1,128)}), f32[8,1,65536]{2,1,0:T(1,128)}, u32[]{:S(2)}, u32[]{:S(2)}) async-start(f32[8,1,65536]{2,1,0:T(1,128)} %broadcast_in_dim.17), calls=%async_computation.11 | async-start | bytes 4194304 | tf_op jit(solution)/shard_map/all_to_all | solution.py:13
  241.6 2.9 fusion.27
  248.4 81.9 %all-reduce.4.cloned.1.call-done = f32[2,64,1920]{2,1,0:T(8,128)} async-done(((f32[2,64,1920]{2,1,0:T(8,128)}), f32[2,64,1920]{2,1,0:T(8,128)}) %all-reduce.4.cloned.1.call-update) | async-done | bytes 983056 | tf_op jit(solution)/shard_map/psum | solution.py:169
  330.3 2.2 broadcast_multiply_fusion
  332.5 3.2 reduce_sum.39
  (78 shorter events, 31.5 us)
Async XLA Ops:
  8.0 33.8 %copy-start = (bf16[1920,512]{1,0:T(8,128)(2,1)S(1)}, bf16[1920,512]{1,0:T(8,128)(2,1)}, u32[]{:S(2)}) copy-start(bf16[1920,512]{1,0:T(8,128)(2,1)} %param.10) | copy-start | bytes 5898244
  8.0 49.9 %reduce-scatter.9.cloned.1.call-start = ((), (), s32[]{:S(2)}) async-start(), calls=%async_computation.14 | async-start | bytes 2457600 | tf_op jit(solution)/shard_map/reduce_scatter | solution.py:48
  20.7 3.4 copy-start.6
  20.7 3.6 %copy-start.2 = (bf16[2,64,1920]{2,1,0:T(8,128)(2,1)S(1)}, bf16[2,64,1920]{2,1,0:T(8,128)(2,1)}, u32[]{:S(2)}) copy-start(bf16[2,64,1920]{2,1,0:T(8,128)(2,1)} %param.12) | copy-start | bytes 1474564
  28.0 69.3 %reduce-scatter.5.cloned.1.call-start = ((), (), s32[]{:S(2)}) async-start(), calls=%async_computation.12 | async-start | bytes 2457600 | tf_op jit(solution)/shard_map/reduce_scatter | solution.py:48
  31.1 115.4 %all-reduce.6.cloned.1.call-start = ((), (), s32[]{:S(2)}) async-start(), calls=%async_computation.17 | async-start | bytes 3932160
  43.8 14.2 %copy-start.8 = (bf16[64,512]{1,0:T(8,128)(2,1)S(1)}, bf16[64,512]{1,0:T(8,128)(2,1)}, u32[]{:S(2)}) copy-start(bf16[64,512]{1,0:T(8,128)(2,1)} %param.14) | copy-start | bytes 196612
  43.8 102.7 %reduce-scatter.11.cloned.1.call-start = ((), (), s32[]{:S(2)}) async-start(), calls=%async_computation.15 | async-start | bytes 614400 | tf_op jit(solution)/shard_map/reduce_scatter | solution.py:48
  58.2 39.2 %copy-start.13 = (u32[128]{0:T(128)S(1)}, u32[128]{0:T(128)}, u32[]{:S(2)}) copy-start(u32[128]{0:T(128)} %constant.41) | copy-start | bytes 1540
  59.2 87.3 %copy-start.9 = (bf16[1920,64]{0,1:T(8,128)(2,1)S(1)}, bf16[1920,64]{0,1:T(8,128)(2,1)}, u32[]{:S(2)}) copy-start(bf16[1920,64]{0,1:T(8,128)(2,1)} %param.13) | copy-start | bytes 737284
  59.3 39.4 %all-to-all-start.4 = ((f32[16,256,64]{1,2,0:T(8,128)}), f32[16,256,64]{1,2,0:T(8,128)}, u32[]{:S(2)}, u32[]{:S(2)}) async-start(f32[16,256,64]{1,2,0:T(8,128)} %broadcast_in_dim.15), calls=%async_computation.8 | async-start | bytes 2097152 | tf_op jit(solution)/shard_map/all_to_all | solution.py:13
  64.7 81.8 %reduce-scatter.7.cloned.1.call-start = ((), (), s32[]{:S(2)}) async-start(), calls=%async_computation.13 | async-start | bytes 614400 | tf_op jit(solution)/shard_map/reduce_scatter | solution.py:48
  99.9 49.7 %copy-start.10 = (bf16[256,64]{0,1:T(8,128)(2,1)}, bf16[256,64]{0,1:T(8,128)(2,1)S(1)}, u32[]{:S(2)}) copy-start(bf16[256,64]{0,1:T(8,128)(2,1)S(1)} %reduce_sum.37) | copy-start | bytes 98308
  149.6 21.1 %all-to-all-start.1 = ((bf16[16,16,1920]{2,1,0:T(8,128)(2,1)}), bf16[16,16,1920]{2,1,0:T(8,128)(2,1)S(1)}, u32[]{:S(2)}, u32[]{:S(2)}) async-start(bf16[16,16,1920]{2,1,0:T(8,128)(2,1)} %broadcast_in_dim.13), calls=%async_computation.5 | async-start | bytes 1966080 | tf_op jit(solution)/shard_map/all_to_all | solution.py:13
  173.1 30.9 %all-to-all-start.5 = ((bf16[16,16,2,1920]{3,1,2,0:T(8,128)(2,1)}), bf16[16,16,2,1920]{3,1,2,0:T(8,128)(2,1)}, u32[]{:S(2)}, u32[]{:S(2)}) async-start(bf16[16,16,2,1920]{3,1,2,0:T(8,128)(2,1)} %broadcast_in_dim.16), calls=%async_computation.9 | async-start | bytes 3932160 | tf_op jit(solution)/shard_map/all_to_all | solution.py:13
  204.0 15.3 %all-to-all-start.2 = ((f32[8,32,512]{2,1,0:T(8,128)}), f32[8,32,512]{2,1,0:T(8,128)}, u32[]{:S(2)}, u32[]{:S(2)}) async-start(f32[8,32,512]{2,1,0:T(8,128)} %bitcast.110), calls=%async_computation.6 | async-start | bytes 1048576 | tf_op jit(solution)/shard_map/all_to_all | solution.py:67
  208.2 3.0 copy-start.3
  210.0 1.3 copy-start.1
  219.3 15.2 %all-to-all-start.6 = ((f32[8,32,512]{2,1,0:T(8,128)}), f32[8,32,512]{2,1,0:T(8,128)}, u32[]{:S(2)}, u32[]{:S(2)}) async-start(f32[8,32,512]{2,1,0:T(8,128)} %fusion.3), calls=%async_computation.10 | async-start | bytes 1048576 | tf_op jit(solution)/shard_map/all_to_all | solution.py:67
  236.9 4.7 %copy-start.5 = (f32[256,128]{0,1:S(1)}, f32[256,128]{0,1}, u32[]{:S(2)}) copy-start(f32[256,128]{0,1} %copy-done.4) | copy-start | bytes 393220
  236.9 95.6 %all-to-all-start.7 = ((f32[8,1,65536]{2,1,0:T(1,128)}), f32[8,1,65536]{2,1,0:T(1,128)}, u32[]{:S(2)}, u32[]{:S(2)}) async-start(f32[8,1,65536]{2,1,0:T(1,128)} %broadcast_in_dim.17), calls=%async_computation.11 | async-start | bytes 4194304 | tf_op jit(solution)/shard_map/all_to_all | solution.py:13
  241.4 3.2 copy-start.11
  241.4 88.9 %all-reduce.4.cloned.1.call-start = ((), (), s32[]{:S(2)}) async-start(), calls=%async_computation.16 | async-start | bytes 1966080 | tf_op jit(solution)/shard_map/psum | solution.py:169
  332.5 4.9 %copy-start.7 = (bf16[2,512,64]{1,2,0:T(8,128)(2,1)S(1)}, bf16[2,512,64]{1,2,0:T(8,128)(2,1)}, u32[]{:S(2)}) copy-start(bf16[2,512,64]{1,2,0:T(8,128)(2,1)} %param.11) | copy-start | bytes 393220
  (2 other events, 1.5 us)
Sparse Core Ops, SparseCore 0:
  28.2 29.7 reduce-scatter.8
  60.3 36.9 reduce-scatter.4
  99.7 21.1 reduce-scatter.10
  123.2 22.1 reduce-scatter.6
Sparse Core Ops, SparseCore 1:
  43.9 102.6 all-reduce.5
  245.8 84.5 all-reduce.3
where the time goes:
time: 347 us; the launch traced here: 345 us
  waiting for transfers between devices  222 us (64%)
  starting transfers between devices  28.8 us (8%)
  matrix products  23.7 us (7%)
  blocking collectives  21.6 us (6%)
  local copies, waits for them, and re-layouts  21.4 us (6%)
  between operations  16.2 us (5%)
  other arithmetic  12 us (3%)
    psum x1, waiting for transfers between devices, per_device(): lax.psum(upper_partial, MP)  81.9 us
    unnamed x7, waiting for transfers between devices  46.7 us
    reduce_scatter x4, waiting for transfers between devices, sum_in_order(): parts = lax.psum_scatter(parts, axes[k], scatter_dimension=0, tiled=True)  46.6 us
    all_to_all x4, waiting for transfers between devices, sent_to_all(): lax.all_to_all(jnp.broadcast_to(array[None], (length, *array.shape)), axi...  37.1 us
    all_to_all x2, blocking collectives, sent_to_all(): lax.all_to_all(jnp.broadcast_to(array[None], (length, *array.shape)), axi...  21.6 us
    all_to_all x4, starting transfers between devices, sent_to_all(): lax.all_to_all(jnp.broadcast_to(array[None], (length, *array.shape)), axi...  19.3 us
    all_to_all x2, waiting for transfers between devices, sum_at_owner(): lax.all_to_all(parts, axis, split_axis=0, concat_axis=0, tiled=True)  9.43 us
    all_to_all x2, starting transfers between devices, sum_at_owner(): lax.all_to_all(parts, axis, split_axis=0, concat_axis=0, tiled=True)  9.07 us
  transfers between devices with their start and end apart: 12, of which 7 were waited for; matrix products, arithmetic and copies ran while one was open for 10% of the time, Pallas kernels for 0%

commit v1 on v0

--- a/solution.py
+++ b/solution.py
@@ -166,7 +166,9 @@
     pre_back = jnp.stack([gate_back, up_back], axis=1).astype(jnp.bfloat16)
     back_all = gathered_copies(pre_back, MP, 0)
     upper_partial = jnp.einsum("tkr,tkf->krf", low_part, back_all.astype(single_float))
-    gate_up_output_factor_gradient = adapter_scale * scale_factor * lax.psum(upper_partial, MP)
+    gate_up_output_factor_gradient = (
+        adapter_scale * scale_factor * lax.psum(lax.psum(upper_partial, "mp_0"), "mp_1")
+    )
     back_low_part = jnp.einsum(
         "tkf,krf->tkr", back_all, gate_up_output_factor, preferred_element_type=single_float
     )

time: 347 us -> 349 us (level)
    psum x1 -> x2, waiting for transfers between devices: 81.9 us -> 83.8 us  [the longest x1 43.4 us: per_device(): lax.psum(lax.psum(upper_partial, 'mp_0'), 'mp_1')]
    unnamed x7 -> x8, waiting for transfers between devices: 46.7 us -> 46.7 us
  transfers between devices with their start and end apart: 12 -> 13, of which waited for: 7 -> 8; matrix products, arithmetic and copies ran while one was open for 10% -> 11% of each run, Pallas kernels for 0% -> 0%
where the time goes in v1:
time: 349 us; the launch traced here: 348 us
  waiting for transfers between devices  224 us (64%)
  starting transfers between devices  28.8 us (8%)
  matrix products  23.7 us (7%)
  blocking collectives  21.6 us (6%)
  local copies, waits for them, and re-layouts  21.4 us (6%)
  between operations  16.5 us (5%)
  other arithmetic  12 us (3%)
    unnamed x8, waiting for transfers between devices  46.7 us
    reduce_scatter x4, waiting for transfers between devices, sum_in_order(): parts = lax.psum_scatter(parts, axes[k], scatter_dimension=0, tiled=True)  46.6 us
    psum x1, waiting for transfers between devices, per_device(): lax.psum(lax.psum(upper_partial, 'mp_0'), 'mp_1')  43.4 us
    psum x1, waiting for transfers between devices, per_device(): lax.psum(upper_partial, 'mp_0')  40.5 us
    all_to_all x4, waiting for transfers between devices, sent_to_all(): lax.all_to_all(jnp.broadcast_to(array[None], (length, *array.shape)), axi...  37.1 us
    all_to_all x2, blocking collectives, sent_to_all(): lax.all_to_all(jnp.broadcast_to(array[None], (length, *array.shape)), axi...  21.6 us
    all_to_all x4, starting transfers between devices, sent_to_all(): lax.all_to_all(jnp.broadcast_to(array[None], (length, *array.shape)), axi...  19.3 us
    all_to_all x2, waiting for transfers between devices, sum_at_owner(): lax.all_to_all(parts, axis, split_axis=0, concat_axis=0, tiled=True)  9.43 us
  transfers between devices with their start and end apart: 13, of which 8 were waited for; matrix products, arithmetic and copies ran while one was open for 11% of the time, Pallas kernels for 0%

profile of v1, /device:TPU:0, one launch (start us, length us, event | category | flops | bytes accessed | tf_op | source)
XLA Modules:
  0.0 347.8 jit_solution(11447502772428553956)
XLA Ops:
  9.0 11.7 %all_to_all.41 = bf16[8,32,512]{2,1,0:T(8,128)(2,1)S(1)} all-to-all(bf16[8,32,512]{2,1,0:T(8,128)(2,1)S(1)} %broadcast_in_dim.12), channel_id=1, replica_groups=mesh['dp'=8,'mp_0'=4,'mp_1'=4] {'dp'}, dimensions={0} | all-to-all | bytes 524288 | tf_op jit(solution)/shard_map/all_to_all | solution.py:13
  20.7 3.4 fusion.22
  28.1 3.0 copy.52
  31.8 9.9 %all_to_all.42 = bf16[8,32,512]{2,1,0:T(8,128)(2,1)S(1)} all-to-all(bf16[8,32,512]{2,1,0:T(8,128)(2,1)S(1)} %broadcast_in_dim.14), channel_id=1, replica_groups=mesh['dp'=8,'mp_0'=4,'mp_1'=4] {'dp'}, dimensions={0} | all-to-all | bytes 524288 | tf_op jit(solution)/shard_map/all_to_all | solution.py:13
  43.8 14.1 %reduce-scatter.9.cloned.1.call-done = f32[4,8,2,1920]{3,1,2,0:T(8,128)} async-done(((f32[16,8,2,1920]{3,1,2,0:T(8,128)}), f32[4,8,2,1920]{3,1,2,0:T(8,128)}) %reduce-scatter.9.cloned.1.call-update) | async-done | bytes 491536 | tf_op jit(solution)/shard_map/reduce_scatter | solution.py:48
  59.3 5.5 %all-to-all-start.4 = ((f32[16,256,64]{1,2,0:T(8,128)}), f32[16,256,64]{1,2,0:T(8,128)}, u32[]{:S(2)}, u32[]{:S(2)}) async-start(f32[16,256,64]{1,2,0:T(8,128)} %broadcast_in_dim.15), calls=%async_computation.8 | async-start | bytes 2097152 | tf_op jit(solution)/shard_map/all_to_all | solution.py:13
  64.8 32.6 %reduce-scatter.5.cloned.1.call-done = f32[4,8,2,1920]{3,1,2,0:T(8,128)} async-done(((f32[16,8,2,1920]{3,1,2,0:T(8,128)}), f32[4,8,2,1920]{3,1,2,0:T(8,128)}) %reduce-scatter.5.cloned.1.call-update) | async-done | bytes 491536 | tf_op jit(solution)/shard_map/reduce_scatter | solution.py:48
  99.9 46.6 %all-reduce.9.cloned.1.call-done = f32[256,1920]{1,0:T(8,128)} async-done(((f32[256,1920]{1,0:T(8,128)}), f32[256,1920]{1,0:T(8,128)}) %all-reduce.9.cloned.1.call-update) | async-done | bytes 1966096
  149.6 4.9 %all-to-all-start.1 = ((bf16[16,16,1920]{2,1,0:T(8,128)(2,1)}), bf16[16,16,1920]{2,1,0:T(8,128)(2,1)S(1)}, u32[]{:S(2)}, u32[]{:S(2)}) async-start(bf16[16,16,1920]{2,1,0:T(8,128)(2,1)} %broadcast_in_dim.13), calls=%async_computation.5 | async-start | bytes 1966080 | tf_op jit(solution)/shard_map/all_to_all | solution.py:13
  156.1 14.7 %all-to-all-done.1 = bf16[16,16,1920]{2,1,0:T(8,128)(2,1)S(1)} async-done(((bf16[16,16,1920]{2,1,0:T(8,128)(2,1)}), bf16[16,16,1920]{2,1,0:T(8,128)(2,1)S(1)}, u32[]{:S(2)}, u32[]{:S(2)}) %all-to-all-start.1) | async-done | bytes 983072 | tf_op jit(solution)/shard_map/all_to_all | solution.py:13
  170.8 2.3 broadcast_in_dim.16
  173.1 4.4 %all-to-all-start.5 = ((bf16[16,16,2,1920]{3,1,2,0:T(8,128)(2,1)}), bf16[16,16,2,1920]{3,1,2,0:T(8,128)(2,1)}, u32[]{:S(2)}, u32[]{:S(2)}) async-start(bf16[16,16,2,1920]{3,1,2,0:T(8,128)(2,1)} %broadcast_in_dim.16), calls=%async_computation.9 | async-start | bytes 3932160 | tf_op jit(solution)/shard_map/all_to_all | solution.py:13
  181.5 22.5 %all-to-all-done.5 = bf16[16,16,2,1920]{3,1,2,0:T(8,128)(2,1)} async-done(((bf16[16,16,2,1920]{3,1,2,0:T(8,128)(2,1)}), bf16[16,16,2,1920]{3,1,2,0:T(8,128)(2,1)}, u32[]{:S(2)}, u32[]{:S(2)}) %all-to-all-start.5) | async-done | bytes 1966112 | tf_op jit(solution)/shard_map/all_to_all | solution.py:13
  204.0 4.3 %all-to-all-start.2 = ((f32[8,32,512]{2,1,0:T(8,128)}), f32[8,32,512]{2,1,0:T(8,128)}, u32[]{:S(2)}, u32[]{:S(2)}) async-start(f32[8,32,512]{2,1,0:T(8,128)} %bitcast.110), calls=%async_computation.6 | async-start | bytes 1048576 | tf_op jit(solution)/shard_map/all_to_all | solution.py:67
  214.5 4.7 %fusion.3 = f32[8,32,512]{2,1,0:T(8,128)} fusion(bf16[8,32,1920,2]{2,1,0,3:T(8,128)(2,1)} %bitcast.96, bf16[2,512,1920]{2,1,0:T(8,128)(2,1)} %param.9), kind=kOutput, calls=%fused_computation.6 | convolution fusion | flops 1006632960 | bytes 6422528 | tf_op jit(solution)/shard_map/tkf,kdf->td/dot_general | solution.py:186
  219.3 4.8 %all-to-all-start.6 = ((f32[8,32,512]{2,1,0:T(8,128)}), f32[8,32,512]{2,1,0:T(8,128)}, u32[]{:S(2)}, u32[]{:S(2)}) async-start(f32[8,32,512]{2,1,0:T(8,128)} %fusion.3), calls=%async_computation.10 | async-start | bytes 1048576 | tf_op jit(solution)/shard_map/all_to_all | solution.py:67
  225.0 9.4 %all-to-all-done.6 = f32[8,32,512]{2,1,0:T(8,128)} async-done(((f32[8,32,512]{2,1,0:T(8,128)}), f32[8,32,512]{2,1,0:T(8,128)}, u32[]{:S(2)}, u32[]{:S(2)}) %all-to-all-start.6) | async-done | bytes 524320 | tf_op jit(solution)/shard_map/all_to_all | solution.py:67
  234.5 2.4 broadcast_in_dim.17
  236.9 4.5 %all-to-all-start.7 = ((f32[8,1,65536]{2,1,0:T(1,128)}), f32[8,1,65536]{2,1,0:T(1,128)}, u32[]{:S(2)}, u32[]{:S(2)}) async-start(f32[8,1,65536]{2,1,0:T(1,128)} %broadcast_in_dim.17), calls=%async_computation.11 | async-start | bytes 4194304 | tf_op jit(solution)/shard_map/all_to_all | solution.py:13
  241.4 2.9 fusion.27
  248.5 40.5 %all-reduce.5.cloned.1.call-done = f32[2,64,1920]{2,1,0:T(8,128)} async-done(((f32[2,64,1920]{2,1,0:T(8,128)}), f32[2,64,1920]{2,1,0:T(8,128)}) %all-reduce.5.cloned.1.call-update) | async-done | bytes 983056 | tf_op jit(solution)/shard_map/psum | solution.py:170
  289.0 3.2 reduce_sum.39
  294.7 43.4 %all-reduce.7.cloned.1.call-done = f32[2,64,1920]{2,1,0:T(8,128)} async-done(((f32[2,64,1920]{2,1,0:T(8,128)}), f32[2,64,1920]{2,1,0:T(8,128)}) %all-reduce.7.cloned.1.call-update) | async-done | bytes 983056 | tf_op jit(solution)/shard_map/psum | solution.py:170
  338.1 2.2 broadcast_multiply_fusion
  (81 shorter events, 33.6 us)
Async XLA Ops:
  8.0 33.8 %copy-start = (bf16[1920,512]{1,0:T(8,128)(2,1)S(1)}, bf16[1920,512]{1,0:T(8,128)(2,1)}, u32[]{:S(2)}) copy-start(bf16[1920,512]{1,0:T(8,128)(2,1)} %param.10) | copy-start | bytes 5898244
  8.0 49.9 %reduce-scatter.9.cloned.1.call-start = ((), (), s32[]{:S(2)}) async-start(), calls=%async_computation.14 | async-start | bytes 2457600 | tf_op jit(solution)/shard_map/reduce_scatter | solution.py:48
  20.7 3.4 copy-start.6
  20.7 3.6 %copy-start.2 = (bf16[2,64,1920]{2,1,0:T(8,128)(2,1)S(1)}, bf16[2,64,1920]{2,1,0:T(8,128)(2,1)}, u32[]{:S(2)}) copy-start(bf16[2,64,1920]{2,1,0:T(8,128)(2,1)} %param.12) | copy-start | bytes 1474564
  28.0 69.3 %reduce-scatter.5.cloned.1.call-start = ((), (), s32[]{:S(2)}) async-start(), calls=%async_computation.12 | async-start | bytes 2457600 | tf_op jit(solution)/shard_map/reduce_scatter | solution.py:48
  31.1 115.4 %all-reduce.9.cloned.1.call-start = ((), (), s32[]{:S(2)}) async-start(), calls=%async_computation.18 | async-start | bytes 3932160
  43.8 14.2 %copy-start.8 = (bf16[64,512]{1,0:T(8,128)(2,1)S(1)}, bf16[64,512]{1,0:T(8,128)(2,1)}, u32[]{:S(2)}) copy-start(bf16[64,512]{1,0:T(8,128)(2,1)} %param.14) | copy-start | bytes 196612
  43.8 102.7 %reduce-scatter.11.cloned.1.call-start = ((), (), s32[]{:S(2)}) async-start(), calls=%async_computation.15 | async-start | bytes 614400 | tf_op jit(solution)/shard_map/reduce_scatter | solution.py:48
  58.2 39.2 %copy-start.13 = (u32[128]{0:T(128)S(1)}, u32[128]{0:T(128)}, u32[]{:S(2)}) copy-start(u32[128]{0:T(128)} %constant.41) | copy-start | bytes 1540
  59.2 87.3 %copy-start.9 = (bf16[1920,64]{0,1:T(8,128)(2,1)S(1)}, bf16[1920,64]{0,1:T(8,128)(2,1)}, u32[]{:S(2)}) copy-start(bf16[1920,64]{0,1:T(8,128)(2,1)} %param.13) | copy-start | bytes 737284
  59.3 39.4 %all-to-all-start.4 = ((f32[16,256,64]{1,2,0:T(8,128)}), f32[16,256,64]{1,2,0:T(8,128)}, u32[]{:S(2)}, u32[]{:S(2)}) async-start(f32[16,256,64]{1,2,0:T(8,128)} %broadcast_in_dim.15), calls=%async_computation.8 | async-start | bytes 2097152 | tf_op jit(solution)/shard_map/all_to_all | solution.py:13
  64.7 81.8 %reduce-scatter.7.cloned.1.call-start = ((), (), s32[]{:S(2)}) async-start(), calls=%async_computation.13 | async-start | bytes 614400 | tf_op jit(solution)/shard_map/reduce_scatter | solution.py:48
  99.9 49.7 %copy-start.10 = (bf16[256,64]{0,1:T(8,128)(2,1)}, bf16[256,64]{0,1:T(8,128)(2,1)S(1)}, u32[]{:S(2)}) copy-start(bf16[256,64]{0,1:T(8,128)(2,1)S(1)} %reduce_sum.37) | copy-start | bytes 98308
  149.6 21.1 %all-to-all-start.1 = ((bf16[16,16,1920]{2,1,0:T(8,128)(2,1)}), bf16[16,16,1920]{2,1,0:T(8,128)(2,1)S(1)}, u32[]{:S(2)}, u32[]{:S(2)}) async-start(bf16[16,16,1920]{2,1,0:T(8,128)(2,1)} %broadcast_in_dim.13), calls=%async_computation.5 | async-start | bytes 1966080 | tf_op jit(solution)/shard_map/all_to_all | solution.py:13
  173.1 30.9 %all-to-all-start.5 = ((bf16[16,16,2,1920]{3,1,2,0:T(8,128)(2,1)}), bf16[16,16,2,1920]{3,1,2,0:T(8,128)(2,1)}, u32[]{:S(2)}, u32[]{:S(2)}) async-start(bf16[16,16,2,1920]{3,1,2,0:T(8,128)(2,1)} %broadcast_in_dim.16), calls=%async_computation.9 | async-start | bytes 3932160 | tf_op jit(solution)/shard_map/all_to_all | solution.py:13
  204.0 15.3 %all-to-all-start.2 = ((f32[8,32,512]{2,1,0:T(8,128)}), f32[8,32,512]{2,1,0:T(8,128)}, u32[]{:S(2)}, u32[]{:S(2)}) async-start(f32[8,32,512]{2,1,0:T(8,128)} %bitcast.110), calls=%async_computation.6 | async-start | bytes 1048576 | tf_op jit(solution)/shard_map/all_to_all | solution.py:67
  208.2 3.0 copy-start.3
  219.3 15.2 %all-to-all-start.6 = ((f32[8,32,512]{2,1,0:T(8,128)}), f32[8,32,512]{2,1,0:T(8,128)}, u32[]{:S(2)}, u32[]{:S(2)}) async-start(f32[8,32,512]{2,1,0:T(8,128)} %fusion.3), calls=%async_computation.10 | async-start | bytes 1048576 | tf_op jit(solution)/shard_map/all_to_all | solution.py:67
  236.9 4.5 %copy-start.5 = (f32[256,128]{0,1:S(1)}, f32[256,128]{0,1}, u32[]{:S(2)}) copy-start(f32[256,128]{0,1} %copy-done.4) | copy-start | bytes 393220
  236.9 52.1 %all-to-all-start.7 = ((f32[8,1,65536]{2,1,0:T(1,128)}), f32[8,1,65536]{2,1,0:T(1,128)}, u32[]{:S(2)}, u32[]{:S(2)}) async-start(f32[8,1,65536]{2,1,0:T(1,128)} %broadcast_in_dim.17), calls=%async_computation.11 | async-start | bytes 4194304 | tf_op jit(solution)/shard_map/all_to_all | solution.py:13
  241.4 3.2 copy-start.11
  241.4 47.6 %all-reduce.5.cloned.1.call-start = ((), (), s32[]{:S(2)}) async-start(), calls=%async_computation.16 | async-start | bytes 1966080 | tf_op jit(solution)/shard_map/psum | solution.py:170
  244.4 93.7 %all-reduce.7.cloned.1.call-start = ((), (), s32[]{:S(2)}) async-start(), calls=%async_computation.17 | async-start | bytes 1966080 | tf_op jit(solution)/shard_map/psum | solution.py:170
  288.9 4.0 %copy-start.7 = (bf16[2,512,64]{1,2,0:T(8,128)(2,1)S(1)}, bf16[2,512,64]{1,2,0:T(8,128)(2,1)}, u32[]{:S(2)}) copy-start(bf16[2,512,64]{1,2,0:T(8,128)(2,1)} %param.11) | copy-start | bytes 393220
  (3 other events, 2.8 us)
Sparse Core Ops, SparseCore 0:
  28.2 29.7 reduce-scatter.8
  60.3 36.9 reduce-scatter.4
  99.7 21.1 reduce-scatter.10
  123.2 22.1 reduce-scatter.6
  244.8 44.0 all-reduce.4
  291.2 46.8 all-reduce.6
Sparse Core Ops, SparseCore 1:
  43.9 102.6 all-reduce.8
